TPU v7x, 32 devices: a whole 2x2x4 slice. The times are simulated.
32 devices in a mesh: row: 4 (over y, x), col: 4 (over z), depth: 2 (over core).
Axes of the slice: x: 2, y: 2, z: 4, core: 2. Of those that a mesh axis runs over, the one named last changes fastest.
Arguments:
- halves: bfloat16 [2, 8192, 16384], P(None, 'row', ('col', 'depth')), may hold values from -6 to 6
- spectrum: float32 [2, 16384], P(None, ('col', 'depth')), as said below
- wanted: int32 [4096], P('col'), may hold values from 0 to 32766, as said below
- fraction: float32 [4096], P('col'), may hold values from 0.05 to 0.95
Outputs:
- eigvec: float32 [2, 8192, 4096], P(None, 'row', ('col', 'depth'))
Inputs may be any that keep to these rules, and one draw needn't show every extreme that they name: Read in the order spectrum[0,0], spectrum[1,0], spectrum[0,1], spectrum[1,1], ... the values rise strictly, each by more than 0.05 over the one before. `wanted`: distinct positions in that merged order of the 32768 eigenvalues.
All inputs are finite; a program needn't handle non-finite values.
Results may differ from a plain program's by a relative error of at most 0.0029.
Values may be sent and summed in bfloat16 or wider, within the bound.
A program may use at most 192 MiB of HBM per device.

v0:
```python
import math
import jax
import jax.numpy as jnp
from jax import lax
from jax.sharding import PartitionSpec as P


def broadcast(shard, axis, root):
    mine = lax.axis_index(axis) == root
    return lax.psum(jnp.where(mine, shard, jnp.zeros_like(shard)), axis)


def root_terms(spectrum_full, wanted):
    ordered = jnp.stack([spectrum_full[0], spectrum_full[1]], axis=1).reshape(-1)
    lower = jnp.take(ordered, wanted)
    upper = jnp.take(ordered, wanted + 1)
    return (lower, upper - lower)


def cauchy_block(seam_part, value_part, lower, width, frac):
    return seam_part[:, :, None] / (
        value_part[:, :, None] - lower[None, None, :] - frac[None, None, :] * width[None, None, :]
    )


def column_norms(seam_full, value_full, lower, width, frac):
    step = seam_full.shape[1] // 8
    total = jnp.zeros(lower.shape, jnp.float32)
    for part in range(8):
        cauchy = cauchy_block(
            seam_full[:, part * step : (part + 1) * step],
            value_full[:, part * step : (part + 1) * step],
            lower,
            width,
            frac,
        )
        total = total + jnp.sum(cauchy * cauchy, axis=(0, 1))
    return jnp.sqrt(total)


def panel_product(piece, seam_part, value_part, lower, width, frac):
    columns = lower.shape[0]
    block = math.gcd(columns, 128)

    def one(index):
        start = index * block
        low = lax.dynamic_slice_in_dim(lower, start, block)
        wid = lax.dynamic_slice_in_dim(width, start, block)
        frc = lax.dynamic_slice_in_dim(frac, start, block)
        cauchy = cauchy_block(seam_part, value_part, low, wid, frc)
        product = jnp.einsum(
            "arh,ahk->ark", piece, cauchy.astype(jnp.bfloat16), preferred_element_type=jnp.float32
        )
        return (product, jnp.zeros((block,), jnp.float32))

    products, sums = lax.map(one, jnp.arange(columns // block))
    product = jnp.transpose(products, (1, 2, 0, 3)).reshape(piece.shape[0], piece.shape[1], columns)
    return (product, sums.reshape(-1))


def body(halves, spectrum, wanted, fraction):
    rows_here = halves.shape[1]
    shard_width = halves.shape[2]
    last = broadcast(halves[0, rows_here - 1], "row", lax.axis_size("row") - 1)
    first = broadcast(halves[1, 0], "row", 0)
    seam = jnp.stack([last, first]).astype(jnp.float32)
    seam_full, value_full = (
        lax.all_gather(seam, ("col", "depth"), axis=1, tiled=True),
        lax.all_gather(spectrum, ("col", "depth"), axis=1, tiled=True),
    )
    lower_col, width_col = root_terms(value_full, wanted)
    ncols = lax.axis_size("col")
    ndepth = lax.axis_size("depth")
    layer = lax.axis_index("depth")
    seam_mine = lax.dynamic_index_in_dim(
        seam_full.reshape(2, ncols, ndepth, shard_width), layer, 2, keepdims=False
    ).reshape(2, ncols * shard_width)
    value_mine = lax.dynamic_index_in_dim(
        value_full.reshape(2, ncols, ndepth, shard_width), layer, 2, keepdims=False
    ).reshape(2, ncols * shard_width)
    share = lower_col.shape[0] // ndepth
    product, sums = panel_product(
        lax.all_gather(halves, "col", axis=2, tiled=True),
        seam_mine,
        value_mine,
        lower_col,
        width_col,
        fraction,
    )
    total = product
    product = lax.psum_scatter(total, "depth", scatter_dimension=2, tiled=True)
    lower_own = lax.dynamic_slice_in_dim(lower_col, layer * share, share)
    width_own = lax.dynamic_slice_in_dim(width_col, layer * share, share)
    frac_own = lax.dynamic_slice_in_dim(fraction, layer * share, share)
    norms = column_norms(seam_full, value_full, lower_own, width_own, frac_own)
    return product / norms[None, None, :]


def solution(mesh):
    in_specs = (P(None, "row", ("col", "depth")), P(None, ("col", "depth")), P("col"), P("col"))
    out_specs = P(None, "row", ("col", "depth"))
    return jax.shard_map(body, mesh=mesh, in_specs=in_specs, out_specs=out_specs, check_vma=False)
```

profile of v0, /device:TPU:0, one launch (start us, length us, event | category | flops | bytes accessed | tf_op | source)
XLA Modules:
  0.0 1443.4 jit_solution(10954515901074154995)
XLA Ops:
  7.3 15.7 %all_gather.10 = f32[2,16384]{1,0:T(2,128)S(1)} all-gather(f32[2,2048]{1,0:T(2,128)S(1)} %copy-done.4), channel_id=1, replica_groups=mesh['row'=4,'col'=4,'depth'=2] {'col','depth'}, dimensions={1}, use_global_device_ids=true | all-gather | bytes 147456 | tf_op jit(solution)/shard_map/all_gather | solution.py:69
  23.7 7.2 copy.11
  30.9 8.2 reshape.75
  39.2 6.2 gather_fusion
  45.3 6.2 gather_fusion.1
  51.5 0.8 fusion.7
  52.3 16.1 %all-reduce = (bf16[1,2048]{1,0:T(2,128)(2,1)S(1)}, bf16[1,2048]{1,0:T(2,128)(2,1)S(1)}) all-reduce(bf16[1,2048]{1,0:T(2,128)(2,1)S(1)} %get-tuple-element.83, bf16[1,2048]{1,0:T(2,128)(2,1)S(1)} %get-tuple-element.82), channel_id=1, replica_groups=mesh['row'=4,'col'=4,'depth'=2] {'row'}, use_global_device_ids=true, to_apply=%region_1.0 | all-reduce | flops 4096 | bytes 16384 | tf_op jit(solution)/shard_map/psum | solution.py:10
  68.5 68.2 %all_gather.9 = f32[2,16384]{1,0:T(2,128)S(1)} all-gather(f32[2,2048]{1,0:T(2,128)S(1)} %maximum_convert_fusion), channel_id=1, replica_groups=mesh['row'=4,'col'=4,'depth'=2] {'col','depth'}, dimensions={1}, use_global_device_ids=true | all-gather | bytes 147456 | tf_op jit(solution)/shard_map/all_gather | solution.py:68
  137.5 985.8 %all-gather.2.cloned.1.call-done = bf16[2,2048,8192]{2,1,0:T(8,128)(2,1)} async-done(((bf16[2,2048,2048]{2,1,0:T(8,128)(2,1)}), bf16[2,2048,8192]{2,1,0:T(8,128)(2,1)}) %all-gather.2.cloned.1.call-update) | async-done | bytes 67108880 | tf_op jit(solution)/shard_map/all_gather | solution.py:83
  1123.3 245.9 %while.10 = (s32[]{:T(128)}, f32[8,2,2048,128]{2,3,1,0:T(8,128)}, f32[2,4,2048]{2,1,0:T(4,128)S(1)}, f32[2,4,2048]{2,1,0:T(4,128)S(1)}, s32[8]{0:T(128)S(1)}, /*...) while((s32[]{:T(128)}, f32[8,2,2048,128]{2,3,1,0:T(8,128)}, ...), condition=%wide.region_3.5_spmd, body=%wide.region_2.4_spmd.sunk | while | flops 8598323200 | bytes 69603520 | solution.py:56
  1124.7 29.3 %fusion.17 = f32[8,2,2048,128]{2,3,1,0:T(8,128)} fusion(f32[8,2,2048,128]{2,3,1,0:T(8,128)} %get-tuple-element.175, s32[]{:T(128)} %get-tuple-element.174, bf16[2,2048,8192]{2,1,0:T(8,128)(2,1)} %get-tuple-element.195, f32[128]{0:T(128)S(1)} %dynamic-slice_multiply_fusion.3, f32[128]{0:T(128)S(1)} %dynamic_slice.47, f32[2,8192]{1,0:T(2,128)S(1)} %bitcast.48, ...), kind=kOutput, calls=%fused_computation.9.clone.1 | convolution fusion | flops 8598323200 | bytes 69338624 | tf_op jit(solution)/shard_map/while/body/eval_jaxpr/arh,ahk->ark/dot_general | solution.py:51
  1155.4 29.3 %fusion.17 = f32[8,2,2048,128]{2,3,1,0:T(8,128)} fusion(f32[8,2,2048,128]{2,3,1,0:T(8,128)} %get-tuple-element.175, s32[]{:T(128)} %get-tuple-element.174, bf16[2,2048,8192]{2,1,0:T(8,128)(2,1)} %get-tuple-element.195, f32[128]{0:T(128)S(1)} %dynamic-slice_multiply_fusion.3, f32[128]{0:T(128)S(1)} %dynamic_slice.47, f32[2,8192]{1,0:T(2,128)S(1)} %bitcast.48, ...), kind=kOutput, calls=%fused_computation.9.clone.1 | convolution fusion | flops 8598323200 | bytes 69338624 | tf_op jit(solution)/shard_map/while/body/eval_jaxpr/arh,ahk->ark/dot_general | solution.py:51
  1186.2 29.3 %fusion.17 = f32[8,2,2048,128]{2,3,1,0:T(8,128)} fusion(f32[8,2,2048,128]{2,3,1,0:T(8,128)} %get-tuple-element.175, s32[]{:T(128)} %get-tuple-element.174, bf16[2,2048,8192]{2,1,0:T(8,128)(2,1)} %get-tuple-element.195, f32[128]{0:T(128)S(1)} %dynamic-slice_multiply_fusion.3, f32[128]{0:T(128)S(1)} %dynamic_slice.47, f32[2,8192]{1,0:T(2,128)S(1)} %bitcast.48, ...), kind=kOutput, calls=%fused_computation.9.clone.1 | convolution fusion | flops 8598323200 | bytes 69338624 | tf_op jit(solution)/shard_map/while/body/eval_jaxpr/arh,ahk->ark/dot_general | solution.py:51
  1216.9 29.3 %fusion.17 = f32[8,2,2048,128]{2,3,1,0:T(8,128)} fusion(f32[8,2,2048,128]{2,3,1,0:T(8,128)} %get-tuple-element.175, s32[]{:T(128)} %get-tuple-element.174, bf16[2,2048,8192]{2,1,0:T(8,128)(2,1)} %get-tuple-element.195, f32[128]{0:T(128)S(1)} %dynamic-slice_multiply_fusion.3, f32[128]{0:T(128)S(1)} %dynamic_slice.47, f32[2,8192]{1,0:T(2,128)S(1)} %bitcast.48, ...), kind=kOutput, calls=%fused_computation.9.clone.1 | convolution fusion | flops 8598323200 | bytes 69338624 | tf_op jit(solution)/shard_map/while/body/eval_jaxpr/arh,ahk->ark/dot_general | solution.py:51
  1247.6 29.3 %fusion.17 = f32[8,2,2048,128]{2,3,1,0:T(8,128)} fusion(f32[8,2,2048,128]{2,3,1,0:T(8,128)} %get-tuple-element.175, s32[]{:T(128)} %get-tuple-element.174, bf16[2,2048,8192]{2,1,0:T(8,128)(2,1)} %get-tuple-element.195, f32[128]{0:T(128)S(1)} %dynamic-slice_multiply_fusion.3, f32[128]{0:T(128)S(1)} %dynamic_slice.47, f32[2,8192]{1,0:T(2,128)S(1)} %bitcast.48, ...), kind=kOutput, calls=%fused_computation.9.clone.1 | convolution fusion | flops 8598323200 | bytes 69338624 | tf_op jit(solution)/shard_map/while/body/eval_jaxpr/arh,ahk->ark/dot_general | solution.py:51
  1278.4 29.3 %fusion.17 = f32[8,2,2048,128]{2,3,1,0:T(8,128)} fusion(f32[8,2,2048,128]{2,3,1,0:T(8,128)} %get-tuple-element.175, s32[]{:T(128)} %get-tuple-element.174, bf16[2,2048,8192]{2,1,0:T(8,128)(2,1)} %get-tuple-element.195, f32[128]{0:T(128)S(1)} %dynamic-slice_multiply_fusion.3, f32[128]{0:T(128)S(1)} %dynamic_slice.47, f32[2,8192]{1,0:T(2,128)S(1)} %bitcast.48, ...), kind=kOutput, calls=%fused_computation.9.clone.1 | convolution fusion | flops 8598323200 | bytes 69338624 | tf_op jit(solution)/shard_map/while/body/eval_jaxpr/arh,ahk->ark/dot_general | solution.py:51
  1309.1 29.4 %fusion.17 = f32[8,2,2048,128]{2,3,1,0:T(8,128)} fusion(f32[8,2,2048,128]{2,3,1,0:T(8,128)} %get-tuple-element.175, s32[]{:T(128)} %get-tuple-element.174, bf16[2,2048,8192]{2,1,0:T(8,128)(2,1)} %get-tuple-element.195, f32[128]{0:T(128)S(1)} %dynamic-slice_multiply_fusion.3, f32[128]{0:T(128)S(1)} %dynamic_slice.47, f32[2,8192]{1,0:T(2,128)S(1)} %bitcast.48, ...), kind=kOutput, calls=%fused_computation.9.clone.1 | convolution fusion | flops 8598323200 | bytes 69338624 | tf_op jit(solution)/shard_map/while/body/eval_jaxpr/arh,ahk->ark/dot_general | solution.py:51
  1339.9 29.3 %fusion.17 = f32[8,2,2048,128]{2,3,1,0:T(8,128)} fusion(f32[8,2,2048,128]{2,3,1,0:T(8,128)} %get-tuple-element.175, s32[]{:T(128)} %get-tuple-element.174, bf16[2,2048,8192]{2,1,0:T(8,128)(2,1)} %get-tuple-element.195, f32[128]{0:T(128)S(1)} %dynamic-slice_multiply_fusion.3, f32[128]{0:T(128)S(1)} %dynamic_slice.47, f32[2,8192]{1,0:T(2,128)S(1)} %bitcast.48, ...), kind=kOutput, calls=%fused_computation.9.clone.1 | convolution fusion | flops 8598323200 | bytes 69338624 | tf_op jit(solution)/shard_map/while/body/eval_jaxpr/arh,ahk->ark/dot_general | solution.py:51
  1369.2 18.1 %copy.12 = f32[2,2048,8,128]{3,2,1,0:T(8,128)} copy(f32[2,2048,8,128]{1,3,0,2:T(8,128)} %bitcast.43) | data formatting | bytes 33554432 | tf_op jit(solution)/shard_map/transpose | solution.py:57
  1387.3 18.0 %reshape.76 = f32[2,2048,1024]{2,1,0:T(8,128)} reshape(f32[2,2048,8,128]{3,2,1,0:T(8,128)} %copy.12) | data formatting | bytes 33554432 | tf_op jit(solution)/shard_map/reshape | solution.py:57
  1405.5 0.7 copy-done.3
  1406.3 16.1 %multiply_reduce_fusion.6 = (f32[512]{0:T(512)S(1)}, f32[512]{0:T(512)S(1)}, f32[512]{0:T(512)S(1)}, f32[512]{0:T(512)S(1)}, f32[512]{0:T(512)S(1)}, /*index=5*/f32[512]{0:T(512)S(1)}, f32[512]{0:T(512)S(1)}, f32[512]{0:T(512)S(1)}) fusion(f32[2,2048]{1,0:T(2,128)S(1)} %get-tuple-element.99, f32[2,2048]{1,0:T(2,128)S(1)} %get-tuple-element.91, ...), kind=kLoop, calls=%fused_computation.17 | loop fusion | flops 83881984 | bytes 282624 | tf_op jit(solution)/shard_map/reduce_sum | solution.py:37
  1422.5 6.2 reduce-scatter.2.cloned.1.call-done
  1428.7 7.9 broadcast_divide_fusion
  (75 shorter events, 9.1 us)
Async XLA Ops:
  6.5 0.8 copy-start.4
  6.5 1116.7 %all-gather.2.cloned.1.call-start = ((), (), s32[]{:S(2)}) async-start(), calls=%async_computation.1 | async-start | bytes 83886080 | tf_op jit(solution)/shard_map/all_gather | solution.py:83
  7.3 1421.4 %reduce-scatter.2.cloned.1.call-start = ((), (), s32[]{:S(2)}) async-start(), calls=%async_computation.2 | async-start | bytes 25165824 | tf_op jit(solution)/shard_map/reduce_scatter | solution.py:91
  23.1 0.6 copy-start
  23.7 15.4 %copy-start.5 = (s32[1024]{0:T(1024)S(1)}, s32[1024]{0:T(1024)}, u32[]{:S(2)}) copy-start(s32[1024]{0:T(1024)} %param.10) | copy-start | bytes 12292
  30.9 1092.4 %copy-start.6 = (f32[1024]{0:T(1024)S(1)}, f32[1024]{0:T(1024)}, u32[]{:S(2)}) copy-start(f32[1024]{0:T(1024)} %param.11) | copy-start | bytes 12292
  136.6 0.7 copy-start.2
  1405.3 0.9 copy-start.3
  1405.4 1.0 copy-start.1
Sparse Core Ops, SparseCore 0:
  8.9 1114.3 all-gather.1
  1405.5 23.1 reduce-scatter.1
where the time goes:
time: 1450 us; the launch traced here: 1440 us
  waiting for transfers between devices  993 us (68%)
  matrix products  235 us (16%)
  blocking collectives  100 us (7%)
  local copies, waits for them, and re-layouts  72.1 us (5%)
  other arithmetic  25.6 us (2%)
    all_gather x1, waiting for transfers between devices, body(): lax.all_gather(halves, 'col', axis=2, tiled=True)  986 us
    dot_general x8, matrix products, one(): jnp.einsum('arh,ahk->ark', piece, cauchy.astype(jnp.bfloat16), preferred_...  235 us
    all_gather x1, blocking collectives, body(): lax.all_gather(seam, ('col', 'depth'), axis=1, tiled=True)  68.2 us
  transfers between devices with their start and end apart: 2, of which 2 were waited for; matrix products, arithmetic and copies ran while one was open for 3% of the time, Pallas kernels for 0%

commit v1 on v0

--- a/solution.py
+++ b/solution.py
@@ -80,7 +80,7 @@
     ).reshape(2, ncols * shard_width)
     share = lower_col.shape[0] // ndepth
     product, sums = panel_product(
-        lax.all_gather(halves, "col", axis=2, tiled=True),
+        jnp.concatenate(lax.all_gather(halves, "col"), axis=2),
         seam_mine,
         value_mine,
         lower_col,

time: 1450 us -> 1490 us (1.028)
  local copies, waits for them, and re-layouts: 72.1 us -> 112 us
  blocking collectives: 100 us -> 127 us
  waiting for transfers between devices: 993 us -> 969 us
    reshape x0 -> x1, local copies, waits for them, and re-layouts: none -> 44.1 us  [body(): jnp.concatenate(lax.all_gather(halves, 'col'), axis=2)]
    all_gather x1, blocking collectives: 68.2 us -> 95.4 us  [body(): lax.all_gather(seam, ('col', 'depth'), axis=1, tiled=True)]
    all_gather x1, waiting for transfers between devices: 986 us -> 962 us  [body(): lax.all_gather(halves, 'col')]
where the time goes in v1:
time: 1490 us
  waiting for transfers between devices  969 us (65%)
  matrix products  235 us (16%)
  blocking collectives  127 us (9%)
  local copies, waits for them, and re-layouts  112 us (8%)
  other arithmetic  25.7 us (2%)
    all_gather x1, waiting for transfers between devices, body(): lax.all_gather(halves, 'col')  962 us
    dot_general x8, matrix products, one(): jnp.einsum('arh,ahk->ark', piece, cauchy.astype(jnp.bfloat16), preferred_...  235 us
    all_gather x1, blocking collectives, body(): lax.all_gather(seam, ('col', 'depth'), axis=1, tiled=True)  95.4 us
    reshape x1, local copies, waits for them, and re-layouts, body(): jnp.concatenate(lax.all_gather(halves, 'col'), axis=2)  44.1 us
  transfers between devices with their start and end apart: 2, of which 2 were waited for; matrix products, arithmetic and copies ran while one was open for 3% of the time, Pallas kernels for 0%

profile of v1, /device:TPU:0, one launch (start us, length us, event | category | flops | bytes accessed | tf_op | source)
XLA Modules:
  0.0 1488.1 jit_solution(8726411407510808642)
XLA Ops:
  7.3 15.7 %all_gather.13 = f32[2,16384]{1,0:T(2,128)S(1)} all-gather(f32[2,2048]{1,0:T(2,128)S(1)} %copy-done.4), channel_id=1, replica_groups=mesh['row'=4,'col'=4,'depth'=2] {'col','depth'}, dimensions={1}, use_global_device_ids=true | all-gather | bytes 147456 | tf_op jit(solution)/shard_map/all_gather | solution.py:69
  23.4 0.8 fusion.7
  24.2 16.1 %all-reduce = (bf16[1,2048]{1,0:T(2,128)(2,1)S(1)}, bf16[1,2048]{1,0:T(2,128)(2,1)S(1)}) all-reduce(bf16[1,2048]{1,0:T(2,128)(2,1)S(1)} %get-tuple-element.83, bf16[1,2048]{1,0:T(2,128)(2,1)S(1)} %get-tuple-element.82), channel_id=1, replica_groups=mesh['row'=4,'col'=4,'depth'=2] {'row'}, use_global_device_ids=true, to_apply=%region_1.0 | all-reduce | flops 4096 | bytes 16384 | tf_op jit(solution)/shard_map/psum | solution.py:10
  40.3 95.4 %all_gather.12 = f32[2,16384]{1,0:T(2,128)S(1)} all-gather(f32[2,2048]{1,0:T(2,128)S(1)} %maximum_convert_fusion), channel_id=1, replica_groups=mesh['row'=4,'col'=4,'depth'=2] {'col','depth'}, dimensions={1}, use_global_device_ids=true | all-gather | bytes 147456 | tf_op jit(solution)/shard_map/all_gather | solution.py:68
  136.7 4.9 copy.17
  141.6 6.9 reshape.81
  148.6 6.2 gather_fusion.1
  154.8 6.2 gather_fusion
  160.9 962.3 %all-gather.3.cloned.1.call-done = bf16[8,2048,2048]{2,1,0:T(8,128)(2,1)} async-done(((bf16[2,2048,2048]{2,1,0:T(8,128)(2,1)}), bf16[8,2048,2048]{2,1,0:T(8,128)(2,1)}) %all-gather.3.cloned.1.call-update) | async-done | bytes 67108880 | tf_op jit(solution)/shard_map/all_gather | solution.py:83
  1123.3 44.1 %copy.24 = bf16[4,2,256,8,2048]{4,3,0,2,1:T(8,128)(2,1)} copy(bf16[4,2,256,8,2048]{4,3,2,1,0:T(8,128)(2,1)} %bitcast.18) | data formatting | bytes 134217728 | tf_op jit(solution)/shard_map/reshape | solution.py:83
  1167.4 246.6 %while.10 = (s32[]{:T(128)}, f32[8,2,2048,128]{2,3,1,0:T(8,128)}, f32[2,4,2048]{2,1,0:T(4,128)S(1)}, f32[2,4,2048]{2,1,0:T(4,128)S(1)}, s32[8]{0:T(128)S(1)}, /*...) while((s32[]{:T(128)}, f32[8,2,2048,128]{2,3,1,0:T(8,128)}, ...), condition=%wide.region_3.5_spmd, body=%wide.region_2.4_spmd.sunk | while | flops 8598323200 | bytes 69603016 | solution.py:56
  1168.9 29.3 %fusion.17 = f32[8,2,2048,128]{2,3,1,0:T(8,128)} fusion(f32[8,2,2048,128]{2,3,1,0:T(8,128)} %get-tuple-element.175, s32[]{:T(128)S(6)} %copy.36, bf16[2,2048,8192]{2,1,0:T(8,128)(2,1)} %get-tuple-element.195, f32[128]{0:T(128)S(1)} %dynamic-slice_multiply_fusion.3, f32[128]{0:T(128)S(1)} %dynamic_slice.47, f32[2,8192]{1,0:T(2,128)S(1)} %bitcast.54, ...), kind=kOutput, calls=%fused_computation.9.clone.1 | convolution fusion | flops 8598323200 | bytes 69338112 | tf_op jit(solution)/shard_map/while/body/eval_jaxpr/arh,ahk->ark/dot_general | solution.py:51
  1199.7 29.3 %fusion.17 = f32[8,2,2048,128]{2,3,1,0:T(8,128)} fusion(f32[8,2,2048,128]{2,3,1,0:T(8,128)} %get-tuple-element.175, s32[]{:T(128)S(6)} %copy.36, bf16[2,2048,8192]{2,1,0:T(8,128)(2,1)} %get-tuple-element.195, f32[128]{0:T(128)S(1)} %dynamic-slice_multiply_fusion.3, f32[128]{0:T(128)S(1)} %dynamic_slice.47, f32[2,8192]{1,0:T(2,128)S(1)} %bitcast.54, ...), kind=kOutput, calls=%fused_computation.9.clone.1 | convolution fusion | flops 8598323200 | bytes 69338112 | tf_op jit(solution)/shard_map/while/body/eval_jaxpr/arh,ahk->ark/dot_general | solution.py:51
  1230.5 29.3 %fusion.17 = f32[8,2,2048,128]{2,3,1,0:T(8,128)} fusion(f32[8,2,2048,128]{2,3,1,0:T(8,128)} %get-tuple-element.175, s32[]{:T(128)S(6)} %copy.36, bf16[2,2048,8192]{2,1,0:T(8,128)(2,1)} %get-tuple-element.195, f32[128]{0:T(128)S(1)} %dynamic-slice_multiply_fusion.3, f32[128]{0:T(128)S(1)} %dynamic_slice.47, f32[2,8192]{1,0:T(2,128)S(1)} %bitcast.54, ...), kind=kOutput, calls=%fused_computation.9.clone.1 | convolution fusion | flops 8598323200 | bytes 69338112 | tf_op jit(solution)/shard_map/while/body/eval_jaxpr/arh,ahk->ark/dot_general | solution.py:51
  1261.3 29.3 %fusion.17 = f32[8,2,2048,128]{2,3,1,0:T(8,128)} fusion(f32[8,2,2048,128]{2,3,1,0:T(8,128)} %get-tuple-element.175, s32[]{:T(128)S(6)} %copy.36, bf16[2,2048,8192]{2,1,0:T(8,128)(2,1)} %get-tuple-element.195, f32[128]{0:T(128)S(1)} %dynamic-slice_multiply_fusion.3, f32[128]{0:T(128)S(1)} %dynamic_slice.47, f32[2,8192]{1,0:T(2,128)S(1)} %bitcast.54, ...), kind=kOutput, calls=%fused_computation.9.clone.1 | convolution fusion | flops 8598323200 | bytes 69338112 | tf_op jit(solution)/shard_map/while/body/eval_jaxpr/arh,ahk->ark/dot_general | solution.py:51
  1292.2 29.4 %fusion.17 = f32[8,2,2048,128]{2,3,1,0:T(8,128)} fusion(f32[8,2,2048,128]{2,3,1,0:T(8,128)} %get-tuple-element.175, s32[]{:T(128)S(6)} %copy.36, bf16[2,2048,8192]{2,1,0:T(8,128)(2,1)} %get-tuple-element.195, f32[128]{0:T(128)S(1)} %dynamic-slice_multiply_fusion.3, f32[128]{0:T(128)S(1)} %dynamic_slice.47, f32[2,8192]{1,0:T(2,128)S(1)} %bitcast.54, ...), kind=kOutput, calls=%fused_computation.9.clone.1 | convolution fusion | flops 8598323200 | bytes 69338112 | tf_op jit(solution)/shard_map/while/body/eval_jaxpr/arh,ahk->ark/dot_general | solution.py:51
  1323.0 29.3 %fusion.17 = f32[8,2,2048,128]{2,3,1,0:T(8,128)} fusion(f32[8,2,2048,128]{2,3,1,0:T(8,128)} %get-tuple-element.175, s32[]{:T(128)S(6)} %copy.36, bf16[2,2048,8192]{2,1,0:T(8,128)(2,1)} %get-tuple-element.195, f32[128]{0:T(128)S(1)} %dynamic-slice_multiply_fusion.3, f32[128]{0:T(128)S(1)} %dynamic_slice.47, f32[2,8192]{1,0:T(2,128)S(1)} %bitcast.54, ...), kind=kOutput, calls=%fused_computation.9.clone.1 | convolution fusion | flops 8598323200 | bytes 69338112 | tf_op jit(solution)/shard_map/while/body/eval_jaxpr/arh,ahk->ark/dot_general | solution.py:51
  1353.8 29.3 %fusion.17 = f32[8,2,2048,128]{2,3,1,0:T(8,128)} fusion(f32[8,2,2048,128]{2,3,1,0:T(8,128)} %get-tuple-element.175, s32[]{:T(128)S(6)} %copy.36, bf16[2,2048,8192]{2,1,0:T(8,128)(2,1)} %get-tuple-element.195, f32[128]{0:T(128)S(1)} %dynamic-slice_multiply_fusion.3, f32[128]{0:T(128)S(1)} %dynamic_slice.47, f32[2,8192]{1,0:T(2,128)S(1)} %bitcast.54, ...), kind=kOutput, calls=%fused_computation.9.clone.1 | convolution fusion | flops 8598323200 | bytes 69338112 | tf_op jit(solution)/shard_map/while/body/eval_jaxpr/arh,ahk->ark/dot_general | solution.py:51
  1384.7 29.3 %fusion.17 = f32[8,2,2048,128]{2,3,1,0:T(8,128)} fusion(f32[8,2,2048,128]{2,3,1,0:T(8,128)} %get-tuple-element.175, s32[]{:T(128)S(6)} %copy.36, bf16[2,2048,8192]{2,1,0:T(8,128)(2,1)} %get-tuple-element.195, f32[128]{0:T(128)S(1)} %dynamic-slice_multiply_fusion.3, f32[128]{0:T(128)S(1)} %dynamic_slice.47, f32[2,8192]{1,0:T(2,128)S(1)} %bitcast.54, ...), kind=kOutput, calls=%fused_computation.9.clone.1 | convolution fusion | flops 8598323200 | bytes 69338112 | tf_op jit(solution)/shard_map/while/body/eval_jaxpr/arh,ahk->ark/dot_general | solution.py:51
  1414.0 18.1 %copy.19 = f32[2,2048,8,128]{3,2,1,0:T(8,128)} copy(f32[2,2048,8,128]{1,3,0,2:T(8,128)} %bitcast.48) | data formatting | bytes 33554432 | tf_op jit(solution)/shard_map/transpose | solution.py:57
  1432.1 18.0 %reshape.84 = f32[2,2048,1024]{2,1,0:T(8,128)} reshape(f32[2,2048,8,128]{3,2,1,0:T(8,128)} %copy.19) | data formatting | bytes 33554432 | tf_op jit(solution)/shard_map/reshape | solution.py:57
  1451.1 16.1 %multiply_reduce_fusion.6 = (f32[512]{0:T(512)S(1)}, f32[512]{0:T(512)S(1)}, f32[512]{0:T(512)S(1)}, f32[512]{0:T(512)S(1)}, f32[512]{0:T(512)S(1)}, /*index=5*/f32[512]{0:T(512)S(1)}, f32[512]{0:T(512)S(1)}, f32[512]{0:T(512)S(1)}) fusion(f32[2,2048]{1,0:T(2,128)S(1)} %get-tuple-element.99, f32[2,2048]{1,0:T(2,128)S(1)} %get-tuple-element.91, ...), kind=kLoop, calls=%fused_computation.17 | loop fusion | flops 83881984 | bytes 282624 | tf_op jit(solution)/shard_map/reduce_sum | solution.py:37
  1467.3 6.2 reduce-scatter.2.cloned.1.call-done
  1473.4 7.9 broadcast_divide_fusion
  (76 shorter events, 9.7 us)
Async XLA Ops:
  6.5 0.8 copy-start.4
  6.5 1116.7 %all-gather.3.cloned.1.call-start = ((), (), s32[]{:S(2)}) async-start(), calls=%async_computation.2 | async-start | bytes 83886080 | tf_op jit(solution)/shard_map/all_gather | solution.py:83
  7.3 1466.2 %reduce-scatter.2.cloned.1.call-start = ((), (), s32[]{:S(2)}) async-start(), calls=%async_computation.1 | async-start | bytes 25165824 | tf_op jit(solution)/shard_map/reduce_scatter | solution.py:91
  23.1 113.6 %copy-start = (f32[2,16384]{1,0:T(2,128)}, f32[2,16384]{1,0:T(2,128)S(1)}, u32[]{:S(2)}) copy-start(f32[2,16384]{1,0:T(2,128)S(1)} %all_gather.13) | copy-start | bytes 393220
  135.7 0.7 copy-start.2
  136.7 11.9 copy-start.5
  1123.3 44.1 %copy-start.6 = (f32[1024]{0:T(1024)S(1)}, f32[1024]{0:T(1024)}, u32[]{:S(2)}) copy-start(f32[1024]{0:T(1024)} %param.11) | copy-start | bytes 12292
  1450.1 0.9 copy-start.3
  1450.2 1.0 copy-start.1
Sparse Core Ops, SparseCore 0:
  8.9 1114.3 all-gather.2
  1450.3 23.0 reduce-scatter.1
